TPU v7x, 256 devices: a 2x2x32 block of a 4x8x32 slice. The times are simulated.
256 devices in a mesh: fields: 4 (over y, x), rows: 64 (over z, core).
Axes of the slice: x: 2, y: 2, z: 32, core: 2. Of those that a mesh axis runs over, the one named last changes fastest.
The devices are a block of a 4x8x32 slice.
Arguments:
- members: bfloat16 [512, 1048576], P('rows', 'fields'), parts along dimension 1, may hold values from -6 to 6
- predicted: bfloat16 [512, 262144], P('rows', 'fields'), parts along dimension 1, may hold values from -16 to 16
- noise: bfloat16 [512, 262144], P('rows', 'fields'), parts along dimension 1, may hold values from -6 to 6
- observed: float32 [262144], P(('fields', 'rows')), parts along dimension 0, may hold values from -12 to 12
- observation_spread: float32 [262144], P(('fields', 'rows')), parts along dimension 0, may hold values from 1 to 16
Outputs:
- updated: bfloat16 [512, 1048576], P('rows', 'fields'), parts along dimension 1
There are 4 independent parts, one for each index of `fields`. A program takes and returns all parts, laid end to end along the dimension named above; each array names one. Nothing has to cross between parts.
All inputs are finite; a program needn't handle non-finite values.
Results may differ from a plain program's by a relative error of at most 0.005.
Values may be sent and summed in bfloat16 or wider, within the bound.
A program may use at most 64 MiB of HBM per device.

v0:
```python
import math

import jax
import jax.numpy as jnp
from jax import lax
from jax.sharding import Mesh
from jax.sharding import PartitionSpec as P

NE = 512
ROWS = ("rows_0", "rows_1")
FIELDS_ROWS = ("fields", "rows_0", "rows_1")


damping = 21.0


def filled_up(lines, length):
    spare = -len(lines) % length
    return jnp.pad(lines, [(0, spare)] + [(0, 0)] * (lines.ndim - 1))


def sum_in_order(parts, axes, order):
    dims = [lax.axis_size(a) for a in axes]
    parts = parts.reshape(*dims, *parts.shape[1:])
    parts = parts.transpose(*order, *range(len(axes), parts.ndim))
    parts = parts.reshape(-1, *parts.shape[len(axes) :])
    for k in order:
        parts = lax.psum_scatter(parts, axes[k], scatter_dimension=0, tiled=True)
    return parts[0]


def stacked_from(array, axes, order):
    parts = array[None]
    for k in order:
        parts = lax.all_gather(parts, axes[k], axis=0, tiled=True)
    block = [lax.axis_size(axes[k]) for k in reversed(order)]
    parts = parts.reshape(*block, *array.shape)
    turned = sorted(range(len(order)), key=lambda place: order[len(order) - 1 - place])
    return parts.transpose(*turned, *range(len(order), parts.ndim)).reshape(-1, *array.shape)


def sum_in_two_steps(array, axes, order):
    length, lines = (lax.axis_size(axes), array.reshape(-1, *array.shape[1:][-1:]))
    parts = filled_up(lines, length).reshape(length, -1, *lines.shape[1:])
    own = sum_in_order(parts, axes, order)
    whole = stacked_from(own, axes, order[::-1]).reshape(-1, *lines.shape[1:])
    return whole[: len(lines)].reshape(array.shape)


def split_up(array, dim, length):
    before, after = (array.shape[:dim], array.shape[dim + 1 :])
    return jnp.moveaxis(array.reshape(*before, length, -1, *after), dim, 0)


def edges_of(length, count):
    unit = 8 if length >= 8 * count else 1
    return [length // unit * k // count * unit for k in range(1, count)]


def laid_out(parts, dim):
    parts = jnp.moveaxis(parts, 0, dim)
    dims = parts.shape
    return parts.reshape(*dims[:dim], dims[dim] * dims[dim + 1], *dims[dim + 2 :])


def several_exchanges(array, axis, pieces, split_dim, concat_dim):
    parts = split_up(array, split_dim, lax.axis_size(axis))
    widest = max(range(1, max(2, parts.ndim - 1)), key=lambda d: parts.shape[d])
    gathered = []
    for slab in jnp.split(parts, edges_of(parts.shape[widest], pieces), axis=widest):
        if slab.size:
            gathered.append(lax.all_to_all(slab, axis, split_axis=0, concat_axis=0, tiled=True))
    return laid_out(jnp.concatenate(gathered, axis=widest), concat_dim)


def on_device(members, predicted, noise, observed, observation_spread):
    row_count = lax.axis_size(ROWS)
    local_count = members.shape[0]
    cells_here = members.shape[1] // row_count
    inverse_square_root = 1.0 / math.sqrt(NE - 1)
    predicted_response, random_jitter = (
        lax.all_to_all(predicted, ROWS, split_axis=1, concat_axis=0, tiled=True),
        lax.all_to_all(noise, ROWS, split_axis=1, concat_axis=0, tiled=True),
    )
    predicted_response = predicted_response.astype(jnp.float32)
    ensemble_data_average = jnp.mean(predicted_response, axis=0)
    standardized_anomalies = (
        (predicted_response - ensemble_data_average) * (inverse_square_root / observation_spread)
    ).astype(jnp.bfloat16)
    measurement_residual = (
        (observed - predicted_response) / observation_spread + random_jitter.astype(jnp.float32)
    ).astype(jnp.bfloat16)
    gram_matrix = lax.dot_general(
        standardized_anomalies,
        standardized_anomalies,
        (((1,), (1,)), ((), ())),
        preferred_element_type=jnp.float32,
    )
    cross_terms = lax.dot_general(
        standardized_anomalies,
        measurement_residual,
        (((1,), (1,)), ((), ())),
        preferred_element_type=jnp.float32,
    )
    identity = jnp.eye(NE, dtype=jnp.float32)
    gram_total, cross_total = (
        sum_in_two_steps(gram_matrix, ROWS, (1, 0)),
        sum_in_two_steps(cross_terms, ROWS, (1, 0)),
    )
    factor = jnp.linalg.cholesky(gram_total + damping * identity)
    weights = jax.scipy.linalg.cho_solve((factor, True), cross_total).astype(jnp.bfloat16)
    blocks = members.reshape(local_count, row_count, cells_here)
    params = lax.all_to_all(blocks, ROWS, split_axis=1, concat_axis=0, tiled=True)[:, 0, :].astype(
        jnp.float32
    )
    cell_mean = jnp.mean(params, axis=0)
    anomaly = ((params - cell_mean) * inverse_square_root).astype(jnp.bfloat16)
    update = lax.dot_general(
        weights, anomaly, (((0,), (0,)), ((), ())), preferred_element_type=jnp.float32
    )
    renewed = (params + update).astype(jnp.bfloat16)[:, None, :]
    result = several_exchanges(renewed, ROWS, 2, 0, 1)
    return result.reshape(local_count, row_count * cells_here)


def solution(mesh):
    split = Mesh(mesh.devices.reshape(mesh.shape["fields"], 32, 2), ("fields", "rows_0", "rows_1"))
    placed = (
        P(ROWS, "fields"),
        P(ROWS, "fields"),
        P(ROWS, "fields"),
        P(FIELDS_ROWS),
        P(FIELDS_ROWS),
    )
    return jax.shard_map(
        on_device, mesh=split, in_specs=placed, out_specs=P(ROWS, "fields"), check_vma=False
    )
```

profile of v0, /device:TPU:37, one launch (start us, length us, event | category | flops | bytes accessed | tf_op | source)
XLA Modules:
  0.0 1349.9 jit_solution(12762346624226458055)
XLA Ops:
  6.5 141.7 %all_to_all.45 = bf16[8,64,1024]{2,0,1:T(8,128)(2,1)S(1)} all-to-all(bf16[8,64,1024]{2,0,1:T(8,128)(2,1)} %bitcast.135), channel_id=1, replica_groups=mesh['fields'=4,'rows_0'=32,'rows_1'=2] {'rows_0','rows_1'}, dimensions={1} | all-to-all | bytes 2097152 | tf_op jit(solution)/shard_map/all_to_all | solution.py:82
  148.3 116.5 %all_to_all.46 = bf16[8,64,1024]{2,0,1:T(8,128)(2,1)S(1)} all-to-all(bf16[8,64,1024]{2,0,1:T(8,128)(2,1)} %bitcast.136), channel_id=1, replica_groups=mesh['fields'=4,'rows_0'=32,'rows_1'=2] {'rows_0','rows_1'}, dimensions={1} | all-to-all | bytes 2097152 | tf_op jit(solution)/shard_map/all_to_all | solution.py:83
  264.8 8.3 all-to-all-start
  273.4 0.3 fusion.10
  273.6 0.7 convolution_bitcast_fusion.1
  274.4 1.1 copy.44
  275.6 0.8 convolution_bitcast_fusion
  276.4 1.1 copy.56
  277.6 27.0 %reduce-scatter.5.cloned.1.call-done = f32[32,8,512]{2,1,0:T(8,128)} async-done(((f32[64,8,512]{2,1,0:T(8,128)}), f32[32,8,512]{2,1,0:T(8,128)}) %reduce-scatter.5.cloned.1.call-update) | async-done | bytes 524304 | tf_op jit(solution)/shard_map/reduce_scatter | solution.py:28
  304.7 29.1 %reduce-scatter.9.cloned.1.call-done = f32[32,8,512]{2,1,0:T(8,128)} async-done(((f32[64,8,512]{2,1,0:T(8,128)}), f32[32,8,512]{2,1,0:T(8,128)}) %reduce-scatter.9.cloned.1.call-update) | async-done | bytes 524304 | tf_op jit(solution)/shard_map/reduce_scatter | solution.py:28
  334.0 176.0 %reduce-scatter.7.cloned.1.call-done = f32[1,8,512]{2,1,0:T(8,128)} async-done(((f32[32,8,512]{2,1,0:T(8,128)}), f32[1,8,512]{2,1,0:T(8,128)}) %reduce-scatter.7.cloned.1.call-update) | async-done | bytes 16400 | tf_op jit(solution)/shard_map/reduce_scatter | solution.py:28
  510.0 182.6 %all_gather.12 = f32[32,8,512]{2,1,0:T(8,128)} all-gather(f32[1,8,512]{2,1,0:T(8,128)} %reduce-scatter.7.cloned.1.call-done), channel_id=1, replica_groups=mesh['fields'=4,'rows_0'=32,'rows_1'=2] {'rows_0'}, dimensions={0}, use_global_device_ids=true | all-gather | bytes 540672 | tf_op jit(solution)/shard_map/all_gather | solution.py:35
  692.7 46.9 %all_gather.14 = f32[32,8,512]{2,1,0:T(8,128)} all-gather(f32[1,8,512]{2,1,0:T(8,128)} %reduce-scatter.11.cloned.1.call-done), channel_id=1, replica_groups=mesh['fields'=4,'rows_0'=32,'rows_1'=2] {'rows_0'}, dimensions={0}, use_global_device_ids=true | all-gather | bytes 540672 | tf_op jit(solution)/shard_map/all_gather | solution.py:35
  739.8 1.3 copy.45
  741.1 0.3 copy.46
  741.5 0.3 copy.47
  741.9 0.2 fusion.16
  742.1 11.7 cholesky.103
  754.0 9.8 custom-call.34
  763.8 0.3 fusion.46
  764.2 0.3 convolution_subtract_fusion.6
  764.6 11.7 cholesky.215
  776.4 10.2 custom-call.35
  786.8 0.3 convolution_dynamic-update-slice_fusion
  787.1 0.6 convolution_subtract_fusion.7
  787.7 11.7 cholesky.236
  799.6 9.8 custom-call.36
  809.4 0.3 convolution_dynamic-update-slice_fusion.1
  809.7 0.5 convolution_subtract_fusion.8
  810.2 11.7 cholesky.253
  822.0 0.7 compare_reduce_fusion.2
  824.0 0.7 compare_reduce_fusion.1
  825.3 0.7 compare_reduce_fusion
  826.8 8.8 while.1
  827.1 0.6 fusion.92
  827.7 1.4 dynamic-slice.7
  829.2 0.6 fusion.92
  829.8 1.4 dynamic-slice.7
  831.4 0.6 fusion.92
  832.0 1.4 dynamic-slice.7
  833.5 0.6 fusion.92
  834.1 1.4 dynamic-slice.7
  835.6 39.3 %custom-call.37 = f32[4,128,128]{1,2,0:T(8,128)S(1)} custom-call(f32[4,128,128]{2,1,0:T(8,128)S(1)} %get-tuple-element.12), custom_call_target="InvertDiagBlocksLowerTriangular" | custom-call | tf_op jit(solution)/shard_map/jit(_cho_solve)/triangular_solve | solution.py:111
  874.9 1.3 fusion.74
  876.3 0.4 fusion.59
  876.7 0.4 convolution_subtract_fusion.3
  877.2 0.4 fusion.61
  877.6 0.5 convolution_subtract_fusion.2
  878.1 0.4 fusion.63
  878.5 0.7 convolution_subtract_fusion.5
  879.2 0.4 fusion.65
  879.6 0.4 fusion.75
  880.0 0.4 convolution_subtract_fusion.1
  880.3 0.4 fusion.76
  880.7 0.4 convolution_subtract_fusion
  881.1 0.4 fusion.77
  881.5 0.6 convolution_subtract_fusion.4
  882.2 0.4 convolution_convert_fusion
  882.5 3.2 convert_reduce_fusion
  885.7 6.2 fusion.5
  891.9 2.3 fusion.73
  894.2 239.9 %all_to_all.47 = bf16[64,4,1,4096]{3,1,2,0:T(4,128)(2,1)S(1)} all-to-all(bf16[64,4,1,4096]{3,1,2,0:T(4,128)(2,1)S(1)} %get-tuple-element.39), channel_id=1, replica_groups=mesh['fields'=4,'rows_0'=32,'rows_1'=2] {'rows_0','rows_1'}, dimensions={0} | all-to-all | bytes 4194304 | tf_op jit(solution)/shard_map/all_to_all | solution.py:72
  1134.1 205.2 %all_to_all.48 = bf16[64,4,1,4096]{3,1,2,0:T(4,128)(2,1)S(1)} all-to-all(bf16[64,4,1,4096]{3,1,2,0:T(4,128)(2,1)S(1)} %get-tuple-element.40), channel_id=1, replica_groups=mesh['fields'=4,'rows_0'=32,'rows_1'=2] {'rows_0','rows_1'}, dimensions={0} | all-to-all | bytes 4194304 | tf_op jit(solution)/shard_map/all_to_all | solution.py:72
  1339.4 3.4 pad_maximum_fusion
  (62 shorter events, 2.8 us)
Async XLA Ops:
  264.8 8.3 copy-start
  264.8 617.8 %all-to-all-start = ((bf16[8,64,4096]{2,0,1:T(8,128)(2,1)}), bf16[8,64,4096]{2,0,1:T(8,128)(2,1)}, u32[]{:S(2)}, u32[]{:S(2)}) async-start(bf16[8,64,4096]{2,0,1:T(8,128)(2,1)} %bitcast.131), calls=%async_computation | async-start | bytes 8388608 | tf_op jit(solution)/shard_map/all_to_all | solution.py:113
  273.1 31.6 %reduce-scatter.5.cloned.1.call-start = ((), (), s32[]{:S(2)}) async-start(), calls=%async_computation.9 | async-start | bytes 1572864 | tf_op jit(solution)/shard_map/reduce_scatter | solution.py:28
  273.3 2.3 copy-start.1
  275.5 58.3 %reduce-scatter.9.cloned.1.call-start = ((), (), s32[]{:S(2)}) async-start(), calls=%async_computation.12 | async-start | bytes 1572864 | tf_op jit(solution)/shard_map/reduce_scatter | solution.py:28
  277.5 232.5 %reduce-scatter.7.cloned.1.call-start = ((), (), s32[]{:S(2)}) async-start(), calls=%async_computation.10 | async-start | bytes 540672 | tf_op jit(solution)/shard_map/reduce_scatter | solution.py:28
  304.7 388.1 %reduce-scatter.11.cloned.1.call-start = ((), (), s32[]{:S(2)}) async-start(), calls=%async_computation.13 | async-start | bytes 540672 | tf_op jit(solution)/shard_map/reduce_scatter | solution.py:28
  333.9 405.9 %all-gather.3.cloned.1.call-start = ((), (), s32[]{:S(2)}) async-start(), calls=%async_computation.11 | async-start | bytes 1572864 | tf_op jit(solution)/shard_map/all_gather | solution.py:35
  692.6 182.3 %all-gather.5.cloned.1.call-start = ((), (), s32[]{:S(2)}) async-start(), calls=%async_computation.14 | async-start | bytes 1572864 | tf_op jit(solution)/shard_map/all_gather | solution.py:35
Sparse Core Ops, SparseCore 0:
  276.4 28.1 reduce-scatter.4
  307.1 26.6 reduce-scatter.8
  336.4 173.5 reduce-scatter.6
  512.3 164.7 reduce-scatter.10
  692.7 34.7 all-gather.2
  739.9 47.8 all-gather.4
where the time goes:
time: 1360 us; the launch traced here: 1350 us
  blocking collectives  933 us (69%)
  waiting for transfers between devices  233 us (17%)
  other arithmetic  126 us (9%)
  local copies, waits for them, and re-layouts  16.9 us (1%)
  between operations  16.8 us (1%)
  matrix products  16.2 us (1%)
    all_to_all x2, blocking collectives, several_exchanges(): lax.all_to_all(slab, axis, split_axis=0, concat_axis=0, tiled=True)  445 us
    reduce_scatter x4, waiting for transfers between devices, sum_in_order(): parts = lax.psum_scatter(parts, axes[k], scatter_dimension=0, tiled=True)  232 us
    all_gather x2, blocking collectives, stacked_from(): parts = lax.all_gather(parts, axes[k], axis=0, tiled=True)  230 us
    all_to_all x1, blocking collectives, on_device(): lax.all_to_all(predicted, ROWS, split_axis=1, concat_axis=0, tiled=True)  142 us
    all_to_all x1, blocking collectives, on_device(): lax.all_to_all(noise, ROWS, split_axis=1, concat_axis=0, tiled=True)  116 us
    another operation x14, other arithmetic, on_device(): factor = jnp.linalg.cholesky(gram_total + damping * identity)  78.8 us
    another operation x3, other arithmetic, on_device(): jax.scipy.linalg.cho_solve((factor, True), cross_total).astype(jnp.bfloat16)  39.5 us
  transfers between devices with their start and end apart: 7, of which 3 were waited for; matrix products, arithmetic and copies ran while one was open for 11% of the time, Pallas kernels for 0%

commit v1 on v0

v1 whole, which is shorter than its diff:
```python
import functools
import math

import jax
import jax.numpy as jnp
from jax import lax
from jax.experimental import pallas as pl
from jax.experimental.pallas import tpu as pltpu
from jax.sharding import PartitionSpec as P

ROWS = "rows"
MESH = pl.DeviceIdType.MESH
DAMPING = 21.0
CHUNKS = 4
BLOCK = 128
F32 = jnp.float32
BF16 = jnp.bfloat16


def drain(ref, sem):
    pltpu.make_async_copy(ref, ref, sem).wait()


def exact_dot(a, b):
    return jnp.dot(a, b, precision=lax.Precision.HIGHEST, preferred_element_type=F32)


def inverse_in_place(block):
    size = block.shape[0]
    lane = lax.broadcasted_iota(jnp.int32, (size, size), 1)
    line = lax.broadcasted_iota(jnp.int32, (size, size), 0)
    lane_row = lax.broadcasted_iota(jnp.int32, (1, size), 1)

    def step(p, carry):
        held = block[...]
        row = block[pl.ds(p, 1), :]
        pivot = 1.0 / jnp.sum(jnp.where(lane_row == p, row, 0.0), axis=1, keepdims=True)
        column = jnp.sum(jnp.where(lane == p, held, 0.0), axis=1, keepdims=True)
        scaled = jnp.where(lane_row == p, pivot, row * pivot)
        column = jnp.where(line[:, :1] == p, -1.0, column)
        kept = jnp.where((lane == p) | (line == p), 0.0, held)
        block[...] = kept - column * scaled
        return carry

    lax.fori_loop(0, size, step, 0)


def kernel(
    n, members, predicted, noise, observed, spread, out,
    pred_in, noise_in, cells_in, cells_out, white, innov, part, part_in,
    sum_right, sum_left, in_right, in_left, total, table, pivots, weights, anomaly,
    own_sem, data_send, data_sem, in_send, in_sem, out_send, out_sem, pair_send, pair_sem,
    rs_send, rs_right, rs_left, ag_send, ag_right, ag_left, weight_send, weight_sem, own_out,
):
    nz = n // 2
    half = nz // 2
    me = lax.axis_index(ROWS)
    z, core = lax.div(me, 2), lax.rem(me, 2)
    local, cells = members.shape[0], members.shape[1] // n
    data = predicted.shape[1] // n
    count = n * local
    width = cells // CHUNKS
    scale = 1.0 / math.sqrt(count - 1)

    def remote(src, dst, send_sem, recv_sem, peer):
        pltpu.make_async_remote_copy(
            src_ref=src, dst_ref=dst, send_sem=send_sem, recv_sem=recv_sem,
            device_id={ROWS: peer}, device_id_type=MESH,
        ).start()

    def to_peers(send):
        def at(shift, other):
            send(lax.rem(z + shift, nz) * 2 + lax.rem(core + other, 2))

        at(half, 0)
        at(half, 1)

        def both_ways(i, carry):
            for other in (0, 1):
                at(half - i, other)
                at(half + i, other)
            return carry

        lax.fori_loop(1, half, both_ways, 0)
        at(0, 1)

    def span(index, size, offset=0):
        return pl.ds(pl.multiple_of(index * size + offset, 128), size)

    barrier = pltpu.get_barrier_semaphore()

    def greet(i, carry):
        pl.semaphore_signal(barrier, inc=1, device_id={ROWS: lax.rem(me + i, n)}, device_id_type=MESH)
        return carry

    lax.fori_loop(1, n, greet, 0)
    own_pred = pltpu.make_async_copy(predicted.at[:, span(me, data)], pred_in.at[me], own_sem.at[0])
    own_noise = pltpu.make_async_copy(noise.at[:, span(me, data)], noise_in.at[me], own_sem.at[1])
    own_cells = pltpu.make_async_copy(members.at[:, span(me, cells)], cells_in.at[me], own_sem.at[2])
    own_pred.start()
    own_noise.start()
    own_cells.start()
    pl.semaphore_wait(barrier, n - 1)

    def send_data(peer):
        remote(predicted.at[:, span(peer, data)], pred_in.at[me], data_send.at[0], data_sem.at[0], peer)
        remote(noise.at[:, span(peer, data)], noise_in.at[me], data_send.at[1], data_sem.at[1], peer)

    def send_cells(k):
        def send(peer):
            remote(
                members.at[:, pl.ds(pl.multiple_of(peer * cells + k * width, 128), width)],
                cells_in.at[me, :, pl.ds(pl.multiple_of(k * width, 128), width)],
                in_send, in_sem.at[k], peer,
            )

        to_peers(send)

    to_peers(send_data)

    @pl.when(core == 0)
    def _():
        send_cells(0)

    own_pred.wait()
    own_noise.wait()
    drain(pred_in.at[pl.ds(0, n - 1)], data_sem.at[0])
    drain(noise_in.at[pl.ds(0, n - 1)], data_sem.at[1])

    def add_rows(i, acc):
        return acc + pred_in[i].astype(F32)

    sums = lax.fori_loop(0, n, add_rows, jnp.zeros((local, data), F32))
    mean = jnp.sum(sums, axis=0, keepdims=True) * (1.0 / count)
    spreads = spread[...]
    factor = scale / spreads
    target = observed[...]

    def standardize(i, carry):
        x = pred_in[pl.ds(2 * i, 2)].astype(F32).reshape(2 * local, data)
        e = noise_in[pl.ds(2 * i, 2)].astype(F32).reshape(2 * local, data)
        rows = pl.ds(pl.multiple_of(2 * local * i, 2 * local), 2 * local)
        white[rows, :] = ((x - mean) * factor).astype(BF16)
        innov[rows, :] = ((target - x) / spreads + e).astype(BF16)
        return carry

    lax.fori_loop(0, n // 2, standardize, 0)
    lines = part.shape[1]
    along = (((1,), (1,)), ((), ()))

    def products(i, carry):
        rows = white[pl.ds(pl.multiple_of(BLOCK * i, BLOCK), BLOCK), :]
        gram = lax.dot_general(rows, white[...], along, preferred_element_type=F32)
        cross = lax.dot_general(rows, innov[...], along, preferred_element_type=F32)
        slabs = pl.ds(i * (BLOCK // lines), BLOCK // lines)
        part[slabs, :, :count] = gram.reshape(BLOCK // lines, lines, count)
        part[slabs, :, count:] = cross.reshape(BLOCK // lines, lines, count)
        return carry

    lax.fori_loop(0, count // BLOCK, products, 0)

    @pl.when(core == 0)
    def _():
        remote(part, part_in, pair_send, pair_sem, me + 1)

        def rest(k, carry):
            send_cells(k)
            return carry

        lax.fori_loop(1, CHUNKS, rest, 0)
        drain(part, pair_send)
        drain(weights, weight_sem)

    @pl.when(core == 1)
    def _():
        drain(part_in, pair_sem)
        right = lax.rem(z + 1, nz) * 2 + 1
        left = lax.rem(z + nz - 1, nz) * 2 + 1

        def pair(j):
            return part[j] + part_in[j]

        def reduce_right(i, first=False):
            j = lax.rem(z + half + nz - i, nz)
            value = pair(j)
            if not first:
                drain(in_right.at[i - 1], rs_right.at[i - 1])
                value = value + in_right[i - 1]
            sum_right[i] = value
            remote(sum_right.at[i], in_right.at[i], rs_send.at[0], rs_right.at[i], right)

        def reduce_left(i, first=False):
            j = lax.rem(z + nz - half + 1 + i, nz)
            value = pair(j)
            if not first:
                drain(in_left.at[i - 1], rs_left.at[i - 1])
                value = value + in_left[i - 1]
            sum_left[i] = value
            remote(sum_left.at[i], in_left.at[i], rs_send.at[1], rs_left.at[i], left)

        reduce_right(0, True)
        reduce_left(0, True)

        def reduce(i, carry):
            reduce_right(i)
            reduce_left(i)
            return carry

        lax.fori_loop(1, half - 1, reduce, 0)
        reduce_right(half - 1)
        drain(in_left.at[half - 2], rs_left.at[half - 2])
        drain(in_right.at[half - 1], rs_right.at[half - 1])
        total[z] = pair(z) + in_left[half - 2] + in_right[half - 1]

        def spread_right(i, first=False):
            j = lax.rem(z + nz - i, nz)
            if not first:
                drain(total.at[j], ag_right.at[i - 1])
            remote(total.at[j], total.at[j], ag_send.at[0], ag_right.at[i], right)

        def spread_left(i, first=False):
            j = lax.rem(z + i, nz)
            if not first:
                drain(total.at[j], ag_left.at[i - 1])
            remote(total.at[j], total.at[j], ag_send.at[1], ag_left.at[i], left)

        spread_right(0, True)
        spread_left(0, True)

        def spread_on(i, carry):
            spread_right(i)
            spread_left(i)
            return carry

        lax.fori_loop(1, half - 1, spread_on, 0)
        spread_right(half - 1)
        drain(total.at[0], ag_left.at[half - 2])
        drain(total.at[0], ag_right.at[half - 1])

        def all_cells(k, carry):
            send_cells(k)
            return carry

        lax.fori_loop(0, CHUNKS, all_cells, 0)

        def unpack(j, carry):
            table[pl.ds(pl.multiple_of(j * lines, lines), lines), :] = total[j]
            return carry

        lax.fori_loop(0, nz, unpack, 0)
        blocks = count // BLOCK
        eye = lax.broadcasted_iota(jnp.int32, (BLOCK, BLOCK), 0) == lax.broadcasted_iota(
            jnp.int32, (BLOCK, BLOCK), 1
        )
        for k in range(blocks):
            here = slice(k * BLOCK, (k + 1) * BLOCK)
            ahead = slice((k + 1) * BLOCK, 2 * count)
            pivots[...] = table[here, here] + jnp.where(eye, DAMPING, 0.0)
            inverse_in_place(pivots)
            table[here, ahead] = exact_dot(pivots[...], table[here, ahead])
            for i in range(k + 1, blocks):
                rows = slice(i * BLOCK, (i + 1) * BLOCK)
                table[rows, ahead] = table[rows, ahead] - exact_dot(table[rows, here], table[here, ahead])
        for k in reversed(range(blocks)):
            here = slice(k * BLOCK, (k + 1) * BLOCK)
            if k < blocks - 1:
                table[here, count:] = table[here, count:] - exact_dot(
                    table[here, (k + 1) * BLOCK : count], table[(k + 1) * BLOCK : count, count:]
                )
        for k in range(blocks):
            here = slice(k * BLOCK, (k + 1) * BLOCK)
            weights[:, here] = table[here, count:].T.astype(BF16)
        remote(weights, weights, weight_send, weight_sem, me - 1)
        drain(weights, weight_send)
        drain(total.at[pl.ds(0, half)], rs_send.at[0])
        drain(total.at[pl.ds(0, half - 1)], rs_send.at[1])
        drain(total.at[pl.ds(0, half)], ag_send.at[0])
        drain(total.at[pl.ds(0, half - 1)], ag_send.at[1])

    own_cells.wait()

    def update(k, carry):
        columns = pl.ds(pl.multiple_of(k * width, 128), width)
        drain(cells_in.at[pl.ds(0, n - 1), :, columns], in_sem.at[k])

        def add_cells(i, acc):
            return acc + cells_in[i, :, columns].astype(F32)

        sums = lax.fori_loop(0, n, add_cells, jnp.zeros((local, width), F32))
        mean = jnp.sum(sums, axis=0, keepdims=True) * (1.0 / count)

        def center(i, inner):
            x = cells_in[pl.ds(2 * i, 2), :, columns].astype(F32).reshape(2 * local, width)
            rows = pl.ds(pl.multiple_of(2 * local * i, 2 * local), 2 * local)
            anomaly[rows, :] = ((x - mean) * scale).astype(BF16)
            return inner

        lax.fori_loop(0, n // 2, center, 0)

        def renew(i, inner):
            rows = pl.ds(pl.multiple_of(BLOCK * i, BLOCK), BLOCK)
            slabs = pl.ds(i * (BLOCK // local), BLOCK // local)
            change = jnp.dot(weights[rows, :], anomaly[...], preferred_element_type=F32)
            x = cells_in[slabs, :, columns].astype(F32)
            cells_out[slabs, :, columns] = (x + change.reshape(x.shape)).astype(BF16)
            return inner

        lax.fori_loop(0, count // BLOCK, renew, 0)

        def send(peer):
            remote(
                cells_out.at[peer, :, columns],
                out.at[:, pl.ds(pl.multiple_of(me * cells + k * width, 128), width)],
                out_send, out_sem, peer,
            )

        to_peers(send)
        return carry

    lax.fori_loop(0, CHUNKS, update, 0)
    mine = pltpu.make_async_copy(cells_out.at[me], out.at[:, span(me, cells)], own_out)
    mine.start()
    drain(pred_in.at[pl.ds(0, n - 1)], data_send.at[0])
    drain(noise_in.at[pl.ds(0, n - 1)], data_send.at[1])
    drain(cells_in.at[pl.ds(0, n - 1)], in_send)
    drain(cells_out.at[pl.ds(0, n - 1)], out_send)
    drain(cells_out.at[pl.ds(0, n - 1)], out_sem)
    mine.wait()


def solution(mesh):
    n = mesh.shape[ROWS]

    def on_device(members, predicted, noise, observed, spread):
        local = members.shape[0]
        count, nz = n * local, n // 2
        cells, data = members.shape[1] // n, predicted.shape[1] // n
        half, lines = nz // 2, count // nz
        slab = (lines, 2 * count)
        anywhere = pl.BlockSpec(memory_space=pltpu.HBM)
        on_chip = pl.BlockSpec(memory_space=pltpu.VMEM)
        dma = pltpu.SemaphoreType.DMA
        return pl.pallas_call(
            functools.partial(kernel, n),
            name="smoother",
            out_shape=jax.ShapeDtypeStruct(members.shape, members.dtype),
            in_specs=[anywhere, anywhere, anywhere, on_chip, on_chip],
            out_specs=anywhere,
            scratch_shapes=[
                pltpu.VMEM((n, local, data), BF16),
                pltpu.VMEM((n, local, data), BF16),
                pltpu.VMEM((n, local, cells), BF16),
                pltpu.VMEM((n, local, cells), BF16),
                pltpu.VMEM((count, data), BF16),
                pltpu.VMEM((count, data), BF16),
                pltpu.VMEM((nz, *slab), F32),
                pltpu.VMEM((nz, *slab), F32),
                pltpu.VMEM((half, *slab), F32),
                pltpu.VMEM((half, *slab), F32),
                pltpu.VMEM((half, *slab), F32),
                pltpu.VMEM((half, *slab), F32),
                pltpu.VMEM((nz, *slab), F32),
                pltpu.VMEM((count, 2 * count), F32),
                pltpu.VMEM((BLOCK, BLOCK), F32),
                pltpu.VMEM((count, count), BF16),
                pltpu.VMEM((count, cells // CHUNKS), BF16),
                dma((3,)), dma((2,)), dma((2,)), dma, dma((CHUNKS,)), dma, dma, dma, dma,
                dma((2,)), dma((half,)), dma((half,)), dma((2,)), dma((half,)), dma((half,)),
                dma, dma, dma,
            ],
            compiler_params=pltpu.CompilerParams(collective_id=0, has_side_effects=True),
        )(members, predicted, noise, observed.reshape(1, data), spread.reshape(1, data))

    placed = (P(ROWS, "fields"), P(ROWS, "fields"), P(ROWS, "fields"), P(("fields", ROWS)), P(("fields", ROWS)))
    return jax.shard_map(
        on_device, mesh=mesh, in_specs=placed, out_specs=P(ROWS, "fields"), check_vma=False
    )
```

time: 1360 us -> 998 us (0.73)
  Pallas kernels: 0 us -> 994 us
  blocking collectives: 933 us -> 0 us
  waiting for transfers between devices: 233 us -> 0 us
  other arithmetic: 126 us -> 0 us
  between operations: 16.8 us -> 0.01 us
  matrix products: 16.2 us -> 0 us
    pallas_call x0 -> x1, Pallas kernels: none -> 994 us  [on_device(): pl.pallas_call(functools.partial(kernel, n), name='smoother', out_shape=j...]
    all_to_all x4 -> x0, blocking collectives: 703 us -> none  [the longest x2 445 us: several_exchanges(): lax.all_to_all(slab, axis, split_axis=0, concat_axis=0, tiled=True)]
    reduce_scatter x4 -> x0, waiting for transfers between devices: 232 us -> none  [sum_in_order(): parts = lax.psum_scatter(parts, axes[k], scatter_dimension=0, tiled=True)]
    all_gather x2 -> x0, blocking collectives: 230 us -> none  [stacked_from(): parts = lax.all_gather(parts, axes[k], axis=0, tiled=True)]
    another operation x17 -> x0, other arithmetic: 118 us -> none  [the longest x14 78.8 us: on_device(): factor = jnp.linalg.cholesky(gram_total + damping * identity)]
  transfers between devices with their start and end apart: 7 -> 0, of which waited for: 3 -> 0; matrix products, arithmetic and copies ran while one was open for 11% -> 0% of each run, Pallas kernels for 0% -> 0%
where the time goes in v1:
time: 998 us
  Pallas kernels  994 us (100%)
    pallas_call x1, Pallas kernels, on_device(): pl.pallas_call(functools.partial(kernel, n), name='smoother', out_shape=j...  994 us

profile of v1, /device:TPU:37, one launch (start us, length us, event | category | flops | bytes accessed | tf_op | source)
XLA Modules:
  0.0 998.1 jit_solution(7946162712592143040)
XLA Ops:
  0.0 994.3 %smoother.1 = bf16[8,262144]{1,0:T(8,128)(2,1)} custom-call(bf16[8,262144]{1,0:T(8,128)(2,1)} %members.1, bf16[8,65536]{1,0:T(8,128)(2,1)} %predicted.1, bf16[8,65536]{1,0:T(8,128)(2,1)} %noise.1, f32[1,1024]{1,0:T(1,128)} %bitcast.2, f32[1,1024]{1,0:T(1,128)} %bitcast.3), custom_call_target="tpu_custom_call" | custom-call | tf_op jit(solution)/shard_map/smoother/pallas_call | solution.py:343
  994.3 3.7 copy.7

commit v2 on v1

v2 whole, which is shorter than its diff:
```python
import functools
import math

import jax
import jax.numpy as jnp
from jax import lax
from jax.experimental import pallas as pl
from jax.experimental.pallas import tpu as pltpu
from jax.sharding import PartitionSpec as P

ROWS = "rows"
MESH = pl.DeviceIdType.MESH
DAMPING = 21.0
CHUNKS = 4
RELAYED = 3
BLOCK = 128
F32 = jnp.float32
BF16 = jnp.bfloat16


def drain(ref, sem):
    pltpu.make_async_copy(ref, ref, sem).wait()


def exact_dot(a, b):
    return jnp.dot(a, b, precision=lax.Precision.HIGHEST, preferred_element_type=F32)


def halves_of(lines):
    first = (lines // 8 + 1) // 2 * 8
    return ((0, first), (first, lines - first))


def inverse_in_place(block):
    size = block.shape[0]
    lane = lax.broadcasted_iota(jnp.int32, (size, size), 1)
    line = lax.broadcasted_iota(jnp.int32, (size, size), 0)
    lane_row = lax.broadcasted_iota(jnp.int32, (1, size), 1)

    def step(p, carry):
        held = block[...]
        row = block[pl.ds(p, 1), :]
        pivot = 1.0 / jnp.sum(jnp.where(lane_row == p, row, 0.0), axis=1, keepdims=True)
        column = jnp.sum(jnp.where(lane == p, held, 0.0), axis=1, keepdims=True)
        scaled = jnp.where(lane_row == p, pivot, row * pivot)
        column = jnp.where(line[:, :1] == p, -1.0, column)
        kept = jnp.where((lane == p) | (line == p), 0.0, held)
        block[...] = kept - column * scaled
        return carry

    lax.fori_loop(0, size, step, 0)


def kernel(
    n, members, predicted, noise, observed, spread, out,
    pred_in, noise_in, cells_in, cells_out, relay, white, innov, part, part_in,
    sum_right, sum_left, in_right, in_left, total, table, pivots, weights, anomaly,
    own_sem, data_send, data_sem, in_send, in_sem, out_send, out_sem, pair_send, pair_sem,
    rs_send, rs_right, rs_left, ag_send, ag_right, ag_left, weight_send, weight_sem,
    relay_send, relay_sem, beside_send, relayed_send, own_out,
):
    nz = n // 2
    half = nz // 2
    me = lax.axis_index(ROWS)
    z, core = lax.div(me, 2), lax.rem(me, 2)
    local, cells = members.shape[0], members.shape[1] // n
    data = predicted.shape[1] // n
    count = n * local
    width = cells // CHUNKS
    scale = 1.0 / math.sqrt(count - 1)
    blocks = count // BLOCK
    lines = part.shape[0] // nz

    def remote(src, dst, send_sem, recv_sem, peer):
        pltpu.make_async_remote_copy(
            src_ref=src, dst_ref=dst, send_sem=send_sem, recv_sem=recv_sem,
            device_id={ROWS: peer}, device_id_type=MESH,
        ).start()

    def to_other_chips(send):
        def at(shift):
            for other in (0, 1):
                send(lax.rem(z + shift, nz) * 2 + lax.rem(core + other, 2))

        at(half)

        def both_ways(i, carry):
            at(half - i)
            at(half + i)
            return carry

        lax.fori_loop(1, half, both_ways, 0)

    def to_peers(send):
        to_other_chips(send)
        send(z * 2 + 1 - core)

    def span(index, size):
        return pl.ds(pl.multiple_of(index * size, 128), size)

    def piece(index, k):
        return pl.ds(pl.multiple_of(index * cells + k * width, 128), width)
    barrier = pltpu.get_barrier_semaphore()

    def greet(i, carry):
        pl.semaphore_signal(barrier, inc=1, device_id={ROWS: lax.rem(me + i, n)}, device_id_type=MESH)
        return carry

    lax.fori_loop(1, n, greet, 0)
    own_pred = pltpu.make_async_copy(predicted.at[:, span(me, data)], pred_in.at[me], own_sem.at[0])
    own_noise = pltpu.make_async_copy(noise.at[:, span(me, data)], noise_in.at[me], own_sem.at[1])
    own_cells = pltpu.make_async_copy(members.at[:, span(me, cells)], cells_in.at[me], own_sem.at[2])
    own_pred.start()
    own_noise.start()
    own_cells.start()
    pl.semaphore_wait(barrier, n - 1)

    def send_data(peer):
        remote(predicted.at[:, span(peer, data)], pred_in.at[me], data_send.at[0], data_sem.at[0], peer)
        remote(noise.at[:, span(peer, data)], noise_in.at[me], data_send.at[1], data_sem.at[1], peer)

    def send_cells(k):
        def send(peer):
            remote(members.at[:, piece(peer, k)], cells_in.at[me, :, piece(0, k)], in_send, in_sem.at[k], peer)

        to_peers(send)

    def pass_cells(k):
        def send(peer):
            remote(relay.at[:, piece(peer, k)], cells_in.at[me + 1, :, piece(0, k)], relayed_send, in_sem.at[k], peer)

        to_other_chips(send)
    to_peers(send_data)

    @pl.when(core == 0)
    def _():
        send_cells(0)

    @pl.when(core == 1)
    def _():
        remote(members, relay, relay_send, relay_sem, me - 1)

        def beside(k, carry):
            remote(
                members.at[:, piece(me - 1, k)], cells_in.at[me, :, piece(0, k)], beside_send, in_sem.at[k], me - 1
            )
            return carry

        lax.fori_loop(0, RELAYED, beside, 0)
    own_pred.wait()
    own_noise.wait()
    drain(pred_in.at[pl.ds(0, n - 1)], data_sem.at[0])
    drain(noise_in.at[pl.ds(0, n - 1)], data_sem.at[1])

    def add_rows(i, acc):
        return acc + pred_in[i].astype(F32)

    sums = lax.fori_loop(0, n, add_rows, jnp.zeros((local, data), F32))
    mean = jnp.sum(sums, axis=0, keepdims=True) * (1.0 / count)
    spreads = spread[...]
    factor = scale / spreads
    target = observed[...]

    def standardize(i, carry):
        x = pred_in[pl.ds(2 * i, 2)].astype(F32).reshape(2 * local, data)
        e = noise_in[pl.ds(2 * i, 2)].astype(F32).reshape(2 * local, data)
        rows = pl.ds(pl.multiple_of(2 * local * i, 2 * local), 2 * local)
        white[rows, :] = ((x - mean) * factor).astype(BF16)
        innov[rows, :] = ((target - x) / spreads + e).astype(BF16)
        return carry

    lax.fori_loop(0, n // 2, standardize, 0)
    along = (((1,), (1,)), ((), ()))
    panels = []
    for i in range(blocks):
        start = sum(2 * blocks - k for k in range(i)) * BLOCK
        panels.append(start)
        rows = white[i * BLOCK : (i + 1) * BLOCK, :]
        gram = lax.dot_general(rows, white[i * BLOCK :, :], along, preferred_element_type=F32)
        cross = lax.dot_general(rows, innov[...], along, preferred_element_type=F32)
        for k in range(blocks - i):
            part[start + k * BLOCK : start + (k + 1) * BLOCK, :] = gram[:, k * BLOCK : (k + 1) * BLOCK]
        start += (blocks - i) * BLOCK
        for k in range(blocks):
            part[start + k * BLOCK : start + (k + 1) * BLOCK, :] = cross[:, k * BLOCK : (k + 1) * BLOCK]

    @pl.when(core == 0)
    def _():
        remote(part, part_in, pair_send, pair_sem, me + 1)
        drain(relay, relay_sem)

        def rest(k, carry):
            pass_cells(k)
            send_cells(k + 1)
            return carry

        lax.fori_loop(0, min(RELAYED, CHUNKS - 1), rest, 0)
        if RELAYED == CHUNKS:
            pass_cells(CHUNKS - 1)
        drain(part, pair_send)
        drain(weights, weight_sem)

    @pl.when(core == 1)
    def _():
        drain(part_in, pair_sem)
        right = lax.rem(z + 1, nz) * 2 + 1
        left = lax.rem(z + nz - 1, nz) * 2 + 1
        halves = halves_of(lines)

        def slab(j, start, size):
            return pl.ds(pl.multiple_of(j * lines + start, 8), size)

        def pair(j, h):
            return part[slab(j, *halves[h]), :] + part_in[slab(j, *halves[h]), :]

        def reduce_one(i, j, h, first, sums, landed, side, sems, peer):
            rows = pl.ds(*halves[h])
            value = pair(j, h)
            if not first:
                drain(landed.at[i - 1, rows], sems.at[h, i - 1])
                value = value + landed[i - 1, rows]
            sums[i, rows] = value
            remote(sums.at[i, rows], landed.at[i, rows], rs_send.at[side], sems.at[h, i], peer)

        def reduce_right(i, h, first=False):
            reduce_one(i, lax.rem(z + half + nz - i, nz), h, first, sum_right, in_right, 0, rs_right, right)

        def reduce_left(i, h, first=False):
            reduce_one(i, lax.rem(z + nz - half + 1 + i, nz), h, first, sum_left, in_left, 1, rs_left, left)

        for h in (0, 1):
            reduce_right(0, h, True)
            reduce_left(0, h, True)

        def reduce(i, carry):
            for h in (0, 1):
                reduce_right(i, h)
                reduce_left(i, h)
            return carry

        lax.fori_loop(1, half - 1, reduce, 0)
        for h in (0, 1):
            reduce_right(half - 1, h)
        for h in (0, 1):
            rows = pl.ds(*halves[h])
            drain(in_left.at[half - 2, rows], rs_left.at[h, half - 2])
            drain(in_right.at[half - 1, rows], rs_right.at[h, half - 1])
            total[slab(z, *halves[h]), :] = pair(z, h) + in_left[half - 2, rows] + in_right[half - 1, rows]

        def spread_one(i, j, h, first, side, sems, peer):
            rows = slab(j, *halves[h])
            if not first:
                drain(total.at[rows], sems.at[h, i - 1])
            remote(total.at[rows], total.at[rows], ag_send.at[side], sems.at[h, i], peer)

        def spread_right(i, h, first=False):
            spread_one(i, lax.rem(z + nz - i, nz), h, first, 0, ag_right, right)

        def spread_left(i, h, first=False):
            spread_one(i, lax.rem(z + i, nz), h, first, 1, ag_left, left)

        for h in (0, 1):
            spread_right(0, h, True)
            spread_left(0, h, True)

        def spread_on(i, carry):
            for h in (0, 1):
                spread_right(i, h)
                spread_left(i, h)
            return carry

        lax.fori_loop(1, half - 1, spread_on, 0)
        for h in (0, 1):
            spread_right(half - 1, h)
        for h in (0, 1):
            drain(total.at[pl.ds(0, halves[h][1])], ag_left.at[h, half - 2])
            drain(total.at[pl.ds(0, halves[h][1])], ag_right.at[h, half - 1])

        def rest(k, carry):
            send_cells(k)
            return carry

        lax.fori_loop(RELAYED, CHUNKS, rest, 0)
        for i in range(blocks):
            for k in range(2 * blocks - i):
                table[i * BLOCK : (i + 1) * BLOCK, (i + k) * BLOCK : (i + k + 1) * BLOCK] = total[
                    panels[i] + k * BLOCK : panels[i] + (k + 1) * BLOCK, :
                ]
        eye = lax.broadcasted_iota(jnp.int32, (BLOCK, BLOCK), 0) == lax.broadcasted_iota(
            jnp.int32, (BLOCK, BLOCK), 1
        )
        for k in range(blocks):
            here = slice(k * BLOCK, (k + 1) * BLOCK)
            ahead = slice((k + 1) * BLOCK, 2 * count)
            pivots[...] = table[here, here] + jnp.where(eye, DAMPING, 0.0)
            inverse_in_place(pivots)
            panel = table[here, ahead]
            scaled = exact_dot(pivots[...], panel)
            for i in range(k + 1, blocks):
                start = (i - k - 1) * BLOCK
                across = panel[:, start : start + BLOCK].T
                rows = slice(i * BLOCK, (i + 1) * BLOCK)
                table[rows, i * BLOCK :] = table[rows, i * BLOCK :] - exact_dot(across, scaled[:, start:])
            table[here, ahead] = scaled
        for k in reversed(range(blocks - 1)):
            here = slice(k * BLOCK, (k + 1) * BLOCK)
            table[here, count:] = table[here, count:] - exact_dot(
                table[here, (k + 1) * BLOCK : count], table[(k + 1) * BLOCK : count, count:]
            )
        for k in range(blocks):
            here = slice(k * BLOCK, (k + 1) * BLOCK)
            weights[:, here] = table[here, count:].T.astype(BF16)
        remote(weights, weights, weight_send, weight_sem, me - 1)

    own_cells.wait()

    def update(k, carry):
        columns = piece(0, k)
        drain(cells_in.at[pl.ds(0, n - 1), :, columns], in_sem.at[k])

        def add_cells(i, acc):
            return acc + cells_in[i, :, columns].astype(F32)

        sums = lax.fori_loop(0, n, add_cells, jnp.zeros((local, width), F32))
        mean = jnp.sum(sums, axis=0, keepdims=True) * (1.0 / count)

        def center(i, inner):
            x = cells_in[pl.ds(2 * i, 2), :, columns].astype(F32).reshape(2 * local, width)
            rows = pl.ds(pl.multiple_of(2 * local * i, 2 * local), 2 * local)
            anomaly[rows, :] = ((x - mean) * scale).astype(BF16)
            return inner

        lax.fori_loop(0, n // 2, center, 0)

        def renew(i, inner):
            rows = pl.ds(pl.multiple_of(BLOCK * i, BLOCK), BLOCK)
            slabs = pl.ds(i * (BLOCK // local), BLOCK // local)
            change = jnp.dot(weights[rows, :], anomaly[...], preferred_element_type=F32)
            x = cells_in[slabs, :, columns].astype(F32)
            cells_out[slabs, :, columns] = (x + change.reshape(x.shape)).astype(BF16)
            return inner

        lax.fori_loop(0, blocks, renew, 0)

        def send(peer):
            remote(cells_out.at[peer, :, columns], out.at[:, piece(me, k)], out_send, out_sem, peer)

        to_peers(send)
        return carry

    lax.fori_loop(0, CHUNKS, update, 0)
    mine = pltpu.make_async_copy(cells_out.at[me], out.at[:, span(me, cells)], own_out)
    mine.start()
    drain(pred_in.at[pl.ds(0, n - 1)], data_send.at[0])
    drain(noise_in.at[pl.ds(0, n - 1)], data_send.at[1])

    @pl.when(core == 0)
    def _():
        drain(cells_in.at[pl.ds(0, n - 1)], in_send)
        drain(cells_in.at[pl.ds(0, n - 2), :, pl.ds(0, RELAYED * width)], relayed_send)

    @pl.when(core == 1)
    def _():
        if RELAYED < CHUNKS:
            drain(cells_in.at[pl.ds(0, n - 1), :, pl.ds(0, (CHUNKS - RELAYED) * width)], in_send)
        drain(members, relay_send)
        drain(cells_in.at[0, :, pl.ds(0, RELAYED * width)], beside_send)
        drain(weights, weight_send)
        drain(total.at[pl.ds(0, half * lines)], rs_send.at[0])
        drain(total.at[pl.ds(0, (half - 1) * lines)], rs_send.at[1])
        drain(total.at[pl.ds(0, half * lines)], ag_send.at[0])
        drain(total.at[pl.ds(0, (half - 1) * lines)], ag_send.at[1])

    drain(cells_out.at[pl.ds(0, n - 1)], out_send)
    drain(cells_out.at[pl.ds(0, n - 1)], out_sem)
    mine.wait()


def solution(mesh):
    n = mesh.shape[ROWS]

    def on_device(members, predicted, noise, observed, spread):
        local = members.shape[0]
        count, nz = n * local, n // 2
        cells, data = members.shape[1] // n, predicted.shape[1] // n
        half, blocks = nz // 2, count // BLOCK
        packed = (blocks * (blocks + 1) // 2 + blocks * blocks) * BLOCK
        lines = packed // nz
        anywhere = pl.BlockSpec(memory_space=pltpu.HBM)
        on_chip = pl.BlockSpec(memory_space=pltpu.VMEM)
        dma = pltpu.SemaphoreType.DMA
        return pl.pallas_call(
            functools.partial(kernel, n),
            name="smoother",
            out_shape=jax.ShapeDtypeStruct(members.shape, members.dtype),
            in_specs=[anywhere, anywhere, anywhere, on_chip, on_chip],
            out_specs=anywhere,
            scratch_shapes=[
                pltpu.VMEM((n, local, data), BF16),
                pltpu.VMEM((n, local, data), BF16),
                pltpu.VMEM((n, local, cells), BF16),
                pltpu.VMEM((n, local, cells), BF16),
                pltpu.VMEM(members.shape, BF16),
                pltpu.VMEM((count, data), BF16),
                pltpu.VMEM((count, data), BF16),
                pltpu.VMEM((packed, BLOCK), F32),
                pltpu.VMEM((packed, BLOCK), F32),
                pltpu.VMEM((half, lines, BLOCK), F32),
                pltpu.VMEM((half, lines, BLOCK), F32),
                pltpu.VMEM((half, lines, BLOCK), F32),
                pltpu.VMEM((half, lines, BLOCK), F32),
                pltpu.VMEM((packed, BLOCK), F32),
                pltpu.VMEM((count, 2 * count), F32),
                pltpu.VMEM((BLOCK, BLOCK), F32),
                pltpu.VMEM((count, count), BF16),
                pltpu.VMEM((count, cells // CHUNKS), BF16),
                dma((3,)), dma((2,)), dma((2,)), dma, dma((CHUNKS,)), dma, dma, dma, dma,
                dma((2,)), dma((2, half)), dma((2, half)), dma((2,)), dma((2, half)), dma((2, half)),
                dma, dma, dma, dma, dma, dma, dma,
            ],
            compiler_params=pltpu.CompilerParams(collective_id=0, has_side_effects=True),
        )(members, predicted, noise, observed.reshape(1, data), spread.reshape(1, data))

    placed = (P(ROWS, "fields"), P(ROWS, "fields"), P(ROWS, "fields"), P(("fields", ROWS)), P(("fields", ROWS)))
    return jax.shard_map(
        on_device, mesh=mesh, in_specs=placed, out_specs=P(ROWS, "fields"), check_vma=False
    )
```

time: 998 us -> 960 us (0.962)
  Pallas kernels: 994 us -> 956 us
    pallas_call x1, Pallas kernels: 994 us -> 956 us  [on_device(): pl.pallas_call(functools.partial(kernel, n), name='smoother', out_shape=j...]
where the time goes in v2:
time: 960 us
  Pallas kernels  956 us (100%)
    pallas_call x1, Pallas kernels, on_device(): pl.pallas_call(functools.partial(kernel, n), name='smoother', out_shape=j...  956 us

profile of v2, /device:TPU:37, one launch (start us, length us, event | category | flops | bytes accessed | tf_op | source)
XLA Modules:
  0.0 960.2 jit_solution(2273124731403098522)
XLA Ops:
  0.0 956.5 %smoother.1 = bf16[8,262144]{1,0:T(8,128)(2,1)} custom-call(bf16[8,262144]{1,0:T(8,128)(2,1)} %members.1, bf16[8,65536]{1,0:T(8,128)(2,1)} %predicted.1, bf16[8,65536]{1,0:T(8,128)(2,1)} %noise.1, f32[1,1024]{1,0:T(1,128)} %bitcast.2, f32[1,1024]{1,0:T(1,128)} %bitcast.3), custom_call_target="tpu_custom_call" | custom-call | tf_op jit(solution)/shard_map/smoother/pallas_call | solution.py:392
  956.5 3.7 copy.7

commit v3 on v2

--- a/solution.py
+++ b/solution.py
@@ -13,6 +13,7 @@
 DAMPING = 21.0
 CHUNKS = 4
 RELAYED = 3
+NEAR = 4
 BLOCK = 128
 F32 = jnp.float32
 BF16 = jnp.bfloat16
@@ -57,7 +58,7 @@
     sum_right, sum_left, in_right, in_left, total, table, pivots, weights, anomaly,
     own_sem, data_send, data_sem, in_send, in_sem, out_send, out_sem, pair_send, pair_sem,
     rs_send, rs_right, rs_left, ag_send, ag_right, ag_left, weight_send, weight_sem,
-    relay_send, relay_sem, beside_send, relayed_send, own_out,
+    relay_send, relay_sem, beside_send, relayed_send, own_out, known_left, known_right,
 ):
     nz = n // 2
     half = nz // 2
@@ -102,18 +103,21 @@
         return pl.ds(pl.multiple_of(index * cells + k * width, 128), width)
     barrier = pltpu.get_barrier_semaphore()
 
-    def greet(i, carry):
-        pl.semaphore_signal(barrier, inc=1, device_id={ROWS: lax.rem(me + i, n)}, device_id_type=MESH)
-        return carry
-
-    lax.fori_loop(1, n, greet, 0)
+    def chip(shift):
+        return lax.rem(z + shift, nz) * 2
+
+    def greet(semaphore, peer):
+        pl.semaphore_signal(semaphore, inc=1, device_id={ROWS: peer}, device_id_type=MESH)
+
+    for peer in (chip(0) + 1 - core, chip(1), chip(1) + 1, chip(nz - 1), chip(nz - 1) + 1):
+        greet(barrier, peer)
     own_pred = pltpu.make_async_copy(predicted.at[:, span(me, data)], pred_in.at[me], own_sem.at[0])
     own_noise = pltpu.make_async_copy(noise.at[:, span(me, data)], noise_in.at[me], own_sem.at[1])
     own_cells = pltpu.make_async_copy(members.at[:, span(me, cells)], cells_in.at[me], own_sem.at[2])
     own_pred.start()
     own_noise.start()
     own_cells.start()
-    pl.semaphore_wait(barrier, n - 1)
+    pl.semaphore_wait(barrier, 5)
 
     def send_data(peer):
         remote(predicted.at[:, span(peer, data)], pred_in.at[me], data_send.at[0], data_sem.at[0], peer)
@@ -130,7 +134,34 @@
             remote(relay.at[:, piece(peer, k)], cells_in.at[me + 1, :, piece(0, k)], relayed_send, in_sem.at[k], peer)
 
         to_other_chips(send)
-    to_peers(send_data)
+    send_data(chip(0) + 1 - core)
+
+    def data_at(shift):
+        for other in (0, 1):
+            send_data(chip(shift) + lax.rem(core + other, 2))
+
+    def widen(i, carry):
+        greet(known_left.at[i - 1], chip(1) + core)
+        greet(known_right.at[i - 1], chip(nz - 1) + core)
+
+        @pl.when(i <= NEAR)
+        def _():
+            data_at(i)
+            data_at(nz - i)
+
+        pl.semaphore_wait(known_left.at[i - 1], 1)
+        pl.semaphore_wait(known_right.at[i - 1], 1)
+        return carry
+
+    lax.fori_loop(1, half, widen, 0)
+    data_at(half)
+
+    def rest_of_data(i, carry):
+        data_at(half - i)
+        data_at(half + i)
+        return carry
+
+    lax.fori_loop(1, half - NEAR, rest_of_data, 0)
 
     @pl.when(core == 0)
     def _():
@@ -417,6 +448,7 @@
                 dma((3,)), dma((2,)), dma((2,)), dma, dma((CHUNKS,)), dma, dma, dma, dma,
                 dma((2,)), dma((2, half)), dma((2, half)), dma((2,)), dma((2, half)), dma((2, half)),
                 dma, dma, dma, dma, dma, dma, dma,
+                pltpu.SemaphoreType.REGULAR((half - 1,)), pltpu.SemaphoreType.REGULAR((half - 1,)),
             ],
             compiler_params=pltpu.CompilerParams(collective_id=0, has_side_effects=True),
         )(members, predicted, noise, observed.reshape(1, data), spread.reshape(1, data))

time: 960 us -> 956 us (level)
  no operation moved by 1% of the time
where the time goes in v3:
time: 956 us; the launch traced here: 955 us
  Pallas kernels  952 us (100%)
    pallas_call x1, Pallas kernels, on_device(): pl.pallas_call(functools.partial(kernel, n), name='smoother', out_shape=j...  952 us

profile of v3, /device:TPU:37, one launch (start us, length us, event | category | flops | bytes accessed | tf_op | source)
XLA Modules:
  0.0 955.4 jit_solution(199087267645255498)
XLA Ops:
  0.0 951.7 %smoother.1 = bf16[8,262144]{1,0:T(8,128)(2,1)} custom-call(bf16[8,262144]{1,0:T(8,128)(2,1)} %members.1, bf16[8,65536]{1,0:T(8,128)(2,1)} %predicted.1, bf16[8,65536]{1,0:T(8,128)(2,1)} %noise.1, f32[1,1024]{1,0:T(1,128)} %bitcast.2, f32[1,1024]{1,0:T(1,128)} %bitcast.3), custom_call_target="tpu_custom_call" | custom-call | tf_op jit(solution)/shard_map/smoother/pallas_call | solution.py:423
  951.7 3.7 copy.7

commit v4 on v3

--- a/solution.py
+++ b/solution.py
@@ -13,7 +13,7 @@
 DAMPING = 21.0
 CHUNKS = 4
 RELAYED = 3
-NEAR = 4
+NEAR = 6
 BLOCK = 128
 F32 = jnp.float32
 BF16 = jnp.bfloat16
@@ -38,18 +38,31 @@
     line = lax.broadcasted_iota(jnp.int32, (size, size), 0)
     lane_row = lax.broadcasted_iota(jnp.int32, (1, size), 1)
 
-    def step(p, carry):
+    line_column = lax.broadcasted_iota(jnp.int32, (size, 1), 0)
+
+    def across(mask, values):
+        return jnp.sum(jnp.where(mask, values, 0.0), axis=1, keepdims=True)
+
+    def step(i, carry):
+        p, q = 2 * i, 2 * i + 1
         held = block[...]
-        row = block[pl.ds(p, 1), :]
-        pivot = 1.0 / jnp.sum(jnp.where(lane_row == p, row, 0.0), axis=1, keepdims=True)
-        column = jnp.sum(jnp.where(lane == p, held, 0.0), axis=1, keepdims=True)
-        scaled = jnp.where(lane_row == p, pivot, row * pivot)
-        column = jnp.where(line[:, :1] == p, -1.0, column)
-        kept = jnp.where((lane == p) | (line == p), 0.0, held)
-        block[...] = kept - column * scaled
+        row_p, row_q = block[pl.ds(p, 1), :], block[pl.ds(q, 1), :]
+        at_p, at_q = lane_row == p, lane_row == q
+        corner, beside = across(at_q, row_p), across(at_p, row_q)
+        pivot_p = 1.0 / across(at_p, row_p)
+        ratio = corner * pivot_p
+        pivot_q = 1.0 / (across(at_q, row_q) - beside * ratio)
+        scaled_p = jnp.where(at_p, pivot_p, row_p * pivot_p)
+        scaled_q = (jnp.where(at_p, 0.0, row_q) - beside * scaled_p) * pivot_q
+        scaled_q = jnp.where(at_q, pivot_q, scaled_q)
+        column_p = jnp.where(line_column == p, -1.0, across(lane == p, held))
+        column_q = jnp.where(line_column == p, 0.0, across(lane == q, held)) - column_p * ratio
+        column_q = jnp.where(line_column == q, -1.0, column_q)
+        kept = jnp.where((lane == p) | (line == p), 0.0, held) - column_p * scaled_p
+        block[...] = jnp.where((lane == q) | (line == q), 0.0, kept) - column_q * scaled_q
         return carry
 
-    lax.fori_loop(0, size, step, 0)
+    lax.fori_loop(0, size // 2, step, 0)
 
 
 def kernel(

time: 956 us -> 952 us (level)
  no operation moved by 1% of the time
where the time goes in v4:
time: 952 us; the launch traced here: 951 us
  Pallas kernels  948 us (100%)
    pallas_call x1, Pallas kernels, on_device(): pl.pallas_call(functools.partial(kernel, n), name='smoother', out_shape=j...  948 us

profile of v4, /device:TPU:37, one launch (start us, length us, event | category | flops | bytes accessed | tf_op | source)
XLA Modules:
  0.0 951.5 jit_solution(1907840303256716532)
XLA Ops:
  0.0 947.7 %smoother.1 = bf16[8,262144]{1,0:T(8,128)(2,1)} custom-call(bf16[8,262144]{1,0:T(8,128)(2,1)} %members.1, bf16[8,65536]{1,0:T(8,128)(2,1)} %predicted.1, bf16[8,65536]{1,0:T(8,128)(2,1)} %noise.1, f32[1,1024]{1,0:T(1,128)} %bitcast.2, f32[1,1024]{1,0:T(1,128)} %bitcast.3), custom_call_target="tpu_custom_call" | custom-call | tf_op jit(solution)/shard_map/smoother/pallas_call | solution.py:436
  947.7 3.7 copy.7

commit v5 on v4

--- a/solution.py
+++ b/solution.py
@@ -436,9 +436,9 @@
         return pl.pallas_call(
             functools.partial(kernel, n),
             name="smoother",
-            out_shape=jax.ShapeDtypeStruct(members.shape, members.dtype),
+            out_shape=pltpu.VMEM(members.shape, members.dtype),
             in_specs=[anywhere, anywhere, anywhere, on_chip, on_chip],
-            out_specs=anywhere,
+            out_specs=on_chip,
             scratch_shapes=[
                 pltpu.VMEM((n, local, data), BF16),
                 pltpu.VMEM((n, local, data), BF16),
@@ -463,7 +463,9 @@
                 dma, dma, dma, dma, dma, dma, dma,
                 pltpu.SemaphoreType.REGULAR((half - 1,)), pltpu.SemaphoreType.REGULAR((half - 1,)),
             ],
-            compiler_params=pltpu.CompilerParams(collective_id=0, has_side_effects=True),
+            compiler_params=pltpu.CompilerParams(
+                collective_id=0, has_side_effects=True, vmem_limit_bytes=59 * 2**20
+            ),
         )(members, predicted, noise, observed.reshape(1, data), spread.reshape(1, data))
 
     placed = (P(ROWS, "fields"), P(ROWS, "fields"), P(ROWS, "fields"), P(("fields", ROWS)), P(("fields", ROWS)))

time: 952 us -> 950 us (level)
  no operation moved by 1% of the time
where the time goes in v5:
time: 950 us
  Pallas kernels  948 us (100%)
    pallas_call x1, Pallas kernels, on_device(): pl.pallas_call(functools.partial(kernel, n), name='smoother', out_shape=p...  948 us

profile of v5, /device:TPU:37, one launch (start us, length us, event | category | flops | bytes accessed | tf_op | source)
XLA Modules:
  0.0 949.7 jit_solution(8986362632793521906)
XLA Ops:
  0.0 947.6 %smoother.1 = bf16[8,262144]{1,0:T(8,128)(2,1)S(1)} custom-call(bf16[8,262144]{1,0:T(8,128)(2,1)} %members.1, bf16[8,65536]{1,0:T(8,128)(2,1)} %predicted.1, bf16[8,65536]{1,0:T(8,128)(2,1)} %noise.1, f32[1,1024]{1,0:T(1,128)} %bitcast.2, f32[1,1024]{1,0:T(1,128)} %bitcast.3), custom_call_target="tpu_custom_call" | custom-call | tf_op jit(solution)/shard_map/smoother/pallas_call | solution.py:436
  947.6 2.0 copy.7
